TPU v7x, 32 devices: a whole 2x2x4 slice. The times are simulated.
32 devices in a mesh: grp: 4 (over x, core), blk: 8 (over z, y).
Axes of the slice: x: 2, y: 2, z: 4, core: 2. Of those that a mesh axis runs over, the one named last changes fastest.
Arguments:
- orbitals: bfloat16 [8192, 4096], P(('blk', 'grp')), may hold values from -0.75 to 0.75
- point_cells: int32 [512], P(('grp', 'blk')), may hold values from 0 to 255
- point_count: int32 [32], P(('grp', 'blk')), may hold values from 1 to 16
Outputs:
- numerators: bfloat16 [8192, 512], P('blk', 'grp')
- gram: float32 [4, 128, 512], P(None, 'blk', 'grp')
Inputs may be any that keep to these rules, and one draw needn't show every extreme that they name: Slots from point_count[d] on of owner d are empty and give zero columns; no slot of an owner past its count is read as live.
All inputs are finite; a program needn't handle non-finite values.
Results may differ from a plain program's by a relative error of at most 0.001.
Values may be sent and summed in bfloat16 or wider, within the bound.
A program may use at most 128 MiB of HBM per device.

v0:
```python
import jax
import jax.numpy as jnp
from jax import lax
from jax.sharding import PartitionSpec as P


def pair_square(left, right):
    product = lax.dot_general(
        left, right, (((1,), (1,)), ((), ())), preferred_element_type=jnp.float32
    )
    return product * product


def per_device(orbitals, point_cells, point_count):
    capacity = point_cells.shape[0]
    group_count = lax.axis_size("grp")
    quarter_len = capacity * lax.axis_size("blk")
    slot_live = (jnp.arange(capacity, dtype=jnp.int32) < point_count[0]).astype(orbitals.dtype)
    own_points = jnp.take(orbitals, point_cells, axis=0) * slot_live[:, None]
    slab_cells = lax.all_gather(orbitals, "grp", axis=0, tiled=True)
    across = lax.all_gather(own_points, "grp", axis=0, tiled=True)
    quarter = lax.all_gather(own_points, "blk", axis=0, tiled=True)
    numerators = pair_square(slab_cells, quarter).astype(jnp.bfloat16)
    gram = pair_square(across, quarter).reshape(group_count, capacity, quarter_len)
    return (numerators, gram)


def solution(mesh):
    in_specs = (P(("blk", "grp"), None), P(("grp", "blk")), P(("grp", "blk")))
    out_specs = (P("blk", "grp"), P(None, "blk", "grp"))
    return jax.shard_map(
        per_device, mesh=mesh, in_specs=in_specs, out_specs=out_specs, check_vma=False
    )
```

profile of v0, /device:TPU:0, one launch (start us, length us, event | category | flops | bytes accessed | tf_op | source)
XLA Modules:
  0.0 128.6 jit_solution(16857152100967714692)
XLA Ops:
  7.2 0.0 all-gather.3.cloned.1.call-start
  7.9 0.7 compare_select_fusion
  8.5 0.7 compare_convert_fusion
  9.2 2.6 %gather_fusion = bf16[16,4096]{1,0:T(8,128)(2,1)S(1)} fusion(bf16[256,4096]{1,0:T(8,128)(2,1)} %param.3, s32[1024]{0:T(1024)S(1)} %pad_clamp_fusion), kind=kCustom, calls=%fused_computation | custom fusion | bytes 262208 | tf_op jit(solution)/shard_map/jit(_take)/gather | solution.py:19
  11.8 0.7 select_multiply_fusion
  12.5 0.0 all-gather.3.cloned.1.call-update
  12.6 0.0 all-gather.5.cloned.1.call-start
  12.6 0.7 all-gather.5.cloned.1.call-update
  13.3 8.9 %all_gather.11 = bf16[64,4096]{1,0:T(8,128)(2,1)S(1)} all-gather(bf16[16,4096]{1,0:T(8,128)(2,1)} %select_multiply_fusion), channel_id=1, replica_groups=mesh['grp'=4,'blk'=8] {'grp'}, dimensions={0}, use_global_device_ids=true | all-gather | bytes 655360 | tf_op jit(solution)/shard_map/all_gather | solution.py:21
  22.2 33.5 %all-gather.3.cloned.1.call-done = bf16[128,4096]{1,0:T(8,128)(2,1)} async-done(((bf16[16,4096]{1,0:T(8,128)(2,1)}), bf16[128,4096]{1,0:T(8,128)(2,1)}) %all-gather.3.cloned.1.call-update) | async-done | bytes 1048592 | tf_op jit(solution)/shard_map/all_gather | solution.py:22
  55.7 2.3 %convolution_multiply_fusion.1 = f32[64,128]{1,0:T(8,128)} fusion(bf16[64,4096]{1,0:T(8,128)(2,1)S(1)} %all_gather.11, bf16[128,4096]{1,0:T(8,128)(2,1)} %all-gather.3.cloned.1.call-done), kind=kOutput, calls=%fused_computation.4 | convolution fusion | flops 67117056 | bytes 1605632 | tf_op jit(solution)/shard_map/dot_general | solution.py:8
  58.1 56.2 %all-gather.5.cloned.1.call-done = bf16[1024,4096]{1,0:T(8,128)(2,1)} async-done(((bf16[256,4096]{1,0:T(8,128)(2,1)}), bf16[1024,4096]{1,0:T(8,128)(2,1)}) %all-gather.5.cloned.1.call-update) | async-done | bytes 8388624 | tf_op jit(solution)/shard_map/all_gather | solution.py:20
  114.3 6.6 %fusion.1 = bf16[1024,128]{0,1:T(8,128)(2,1)S(1)} fusion(bf16[128,4096]{1,0:T(8,128)(2,1)} %all-gather.3.cloned.1.call-done, bf16[1024,4096]{1,0:T(8,128)(2,1)} %all-gather.5.cloned.1.call-done), kind=kOutput, calls=%fused_computation.3 | convolution fusion | flops 1074003968 | bytes 9699328 | tf_op jit(solution)/shard_map/dot_general | solution.py:8
  120.9 0.8 copy.5
  (1 shorter events, 0.0 us)
Async XLA Ops:
  7.2 48.6 %all-gather.3.cloned.1.call-start = ((), (), s32[]{:S(2)}) async-start(), calls=%async_computation | async-start | bytes 1179648 | tf_op jit(solution)/shard_map/all_gather | solution.py:22
  12.6 101.7 %all-gather.5.cloned.1.call-start = ((), (), s32[]{:S(2)}) async-start(), calls=%async_computation.1 | async-start | bytes 10485760 | tf_op jit(solution)/shard_map/all_gather | solution.py:20
Sparse Core Ops, SparseCore 0:
  12.7 42.9 all-gather.2
  57.3 56.9 all-gather.4
where the time goes:
time: 129 us
  waiting for transfers between devices  90.5 us (70%)
  between operations  14.7 us (11%)
  matrix products  8.94 us (7%)
  blocking collectives  8.86 us (7%)
  local copies, waits for them, and re-layouts  3.45 us (3%)
  other arithmetic  2.07 us (2%)
    all_gather x1, waiting for transfers between devices, per_device(): slab_cells = lax.all_gather(orbitals, 'grp', axis=0, tiled=True)  56.2 us
    all_gather x1, waiting for transfers between devices, per_device(): quarter = lax.all_gather(own_points, 'blk', axis=0, tiled=True)  33.5 us
    dot_general x2, matrix products, pair_square(): lax.dot_general(left, right, (((1,), (1,)), ((), ())), preferred_element_...  8.94 us
    all_gather x1, blocking collectives, per_device(): across = lax.all_gather(own_points, 'grp', axis=0, tiled=True)  8.86 us
    gather x1, local copies, waits for them, and re-layouts, per_device(): own_points = jnp.take(orbitals, point_cells, axis=0) * slot_live[:, None]  2.61 us
  transfers between devices with their start and end apart: 2, of which 2 were waited for; matrix products, arithmetic and copies ran while one was open for 2% of the time, Pallas kernels for 0%

commit v1 on v0

--- a/solution.py
+++ b/solution.py
@@ -12,16 +12,23 @@
 
 
 def per_device(orbitals, point_cells, point_count):
+    cells, width = orbitals.shape
     capacity = point_cells.shape[0]
-    group_count = lax.axis_size("grp")
-    quarter_len = capacity * lax.axis_size("blk")
+    groups = lax.axis_size("grp")
+    blocks = lax.axis_size("blk")
+    quarter_len = capacity * blocks
     slot_live = (jnp.arange(capacity, dtype=jnp.int32) < point_count[0]).astype(orbitals.dtype)
     own_points = jnp.take(orbitals, point_cells, axis=0) * slot_live[:, None]
-    slab_cells = lax.all_gather(orbitals, "grp", axis=0, tiled=True)
-    across = lax.all_gather(own_points, "grp", axis=0, tiled=True)
-    quarter = lax.all_gather(own_points, "blk", axis=0, tiled=True)
-    numerators = pair_square(slab_cells, quarter).astype(jnp.bfloat16)
-    gram = pair_square(across, quarter).reshape(group_count, capacity, quarter_len)
+    points = lax.all_gather(own_points, ("grp", "blk"), axis=0, tiled=True)
+    mine = pair_square(orbitals, points).astype(jnp.bfloat16)
+    mine = mine.reshape(cells, groups, quarter_len).transpose(1, 0, 2)
+    numerators = lax.all_to_all(mine, "grp", 0, 0, tiled=True).reshape(groups * cells, quarter_len)
+    by_owner = points.reshape(groups, blocks, capacity, width)
+    across = lax.dynamic_index_in_dim(by_owner, lax.axis_index("blk"), 1, keepdims=False)
+    quarter = lax.dynamic_index_in_dim(by_owner, lax.axis_index("grp"), 0, keepdims=False)
+    gram = pair_square(
+        across.reshape(groups * capacity, width), quarter.reshape(quarter_len, width)
+    ).reshape(groups, capacity, quarter_len)
     return (numerators, gram)
 
 

time: 129 us -> 101 us (0.78)
  waiting for transfers between devices: 90.5 us -> 69.2 us
  blocking collectives: 8.86 us -> 0 us
  starting transfers between devices: 0.08 us -> 3.44 us
  matrix products: 8.94 us -> 6.31 us
    all_gather x2 -> x1, waiting for transfers between devices: 89.8 us -> 65.4 us  [per_device(): points = lax.all_gather(own_points, ('grp', 'blk'), axis=0, tiled=True)]
    all_gather x1 -> x0, blocking collectives: 8.86 us -> none  [per_device(): across = lax.all_gather(own_points, 'grp', axis=0, tiled=True)]
    all_to_all x0 -> x1, waiting for transfers between devices: none -> 3.83 us  [per_device(): lax.all_to_all(mine, 'grp', 0, 0, tiled=True)]
    all_to_all x0 -> x1, starting transfers between devices: none -> 3.41 us  [per_device(): lax.all_to_all(mine, 'grp', 0, 0, tiled=True)]
    dynamic_slice x0 -> x2, local copies, waits for them, and re-layouts: none -> 3.18 us  [the longest x1 1.89 us: per_device(): lax.dynamic_index_in_dim(by_owner, lax.axis_index('blk'), 1, keepdims=False)]
    dot_general x2, matrix products: 8.94 us -> 6.31 us  [pair_square(): lax.dot_general(left, right, (((1,), (1,)), ((), ())), preferred_element_...]
    gather x1, local copies, waits for them, and re-layouts: 2.61 us -> 0.63 us  [per_device(): own_points = jnp.take(orbitals, point_cells, axis=0) * slot_live[:, None]]
where the time goes in v1:
time: 101 us
  waiting for transfers between devices  69.2 us (69%)
  between operations  14.9 us (15%)
  matrix products  6.31 us (6%)
  local copies, waits for them, and re-layouts  4.66 us (5%)
  starting transfers between devices  3.44 us (3%)
  other arithmetic  2.07 us (2%)
    all_gather x1, waiting for transfers between devices, per_device(): points = lax.all_gather(own_points, ('grp', 'blk'), axis=0, tiled=True)  65.4 us
    dot_general x2, matrix products, pair_square(): lax.dot_general(left, right, (((1,), (1,)), ((), ())), preferred_element_...  6.31 us
    all_to_all x1, waiting for transfers between devices, per_device(): lax.all_to_all(mine, 'grp', 0, 0, tiled=True)  3.83 us
    all_to_all x1, starting transfers between devices, per_device(): lax.all_to_all(mine, 'grp', 0, 0, tiled=True)  3.41 us
  transfers between devices with their start and end apart: 2, of which 2 were waited for; matrix products, arithmetic and copies ran while one was open for 2% of the time, Pallas kernels for 0%

profile of v1, /device:TPU:0, one launch (start us, length us, event | category | flops | bytes accessed | tf_op | source)
XLA Modules:
  0.0 100.5 jit_solution(12332947483019921587)
XLA Ops:
  7.2 0.0 copy-start
  7.2 0.0 all-gather.2.cloned.1.call-start
  8.0 0.7 compare_select_fusion
  8.7 0.7 compare_convert_fusion
  9.3 0.0 copy-done
  9.4 0.6 gather_fusion
  10.0 0.7 select_multiply_fusion
  10.7 0.0 all-gather.2.cloned.1.call-update
  10.8 65.4 %all-gather.2.cloned.1.call-done = bf16[512,4096]{1,0:T(8,128)(2,1)} async-done(((bf16[16,4096]{1,0:T(8,128)(2,1)}), bf16[512,4096]{1,0:T(8,128)(2,1)}) %all-gather.2.cloned.1.call-update) | async-done | bytes 4194320 | tf_op jit(solution)/shard_map/all_gather | solution.py:22
  76.1 1.3 %constant_dynamic-slice_fusion = bf16[1,8,16,4096]{3,2,1,0:T(8,128)(2,1)S(1)} fusion(bf16[4,8,16,4096]{3,2,1,0:T(8,128)(2,1)} %bitcast.18, s32[]{:T(128)S(6)} %select_n.20), kind=kLoop, calls=%fused_computation.9 | loop fusion | bytes 2097156 | tf_op jit(solution)/shard_map/jit(dynamic_index_in_dim)/dynamic_slice | solution.py:28
  77.4 1.9 %constant_dynamic-slice_fusion.1 = bf16[4,1,16,4096]{3,2,1,0:T(8,128)(2,1)} fusion(bf16[4,8,16,4096]{3,2,1,0:T(8,128)(2,1)} %bitcast.19, s32[]{:T(128)S(6)} %select_n.19), kind=kLoop, calls=%fused_computation.10 | loop fusion | bytes 1048580 | tf_op jit(solution)/shard_map/jit(dynamic_index_in_dim)/dynamic_slice | solution.py:27
  79.3 4.2 %fusion = bf16[512,256]{1,0:T(8,128)(2,1)} fusion(bf16[512,4096]{1,0:T(8,128)(2,1)} %all-gather.2.cloned.1.call-done, bf16[256,4096]{1,0:T(8,128)(2,1)S(1)} %copy-done), kind=kOutput, calls=%fused_computation.2 | convolution fusion | flops 1074003968 | bytes 6553600 | tf_op jit(solution)/shard_map/dot_general | solution.py:8
  83.5 3.4 %all-to-all-start = ((bf16[4,256,128]{1,2,0:T(8,128)(2,1)}), bf16[4,256,128]{1,2,0:T(8,128)(2,1)S(1)}, u32[]{:S(2)}, u32[]{:S(2)}) async-start(bf16[4,256,128]{1,2,0:T(8,128)(2,1)} %bitcast.20), calls=%async_computation | async-start | bytes 524288 | tf_op jit(solution)/shard_map/all_to_all | solution.py:25
  86.9 2.1 %convolution_multiply_fusion.1 = f32[64,128]{1,0:T(8,128)} fusion(bf16[64,4096]{1,0:T(8,128)(2,1)} %bitcast.17, bf16[128,4096]{1,0:T(8,128)(2,1)S(1)} %bitcast.16), kind=kOutput, calls=%fused_computation.3 | convolution fusion | flops 67117056 | bytes 1605632 | tf_op jit(solution)/shard_map/dot_general | solution.py:8
  89.0 3.8 %all-to-all-done = bf16[4,256,128]{1,2,0:T(8,128)(2,1)S(1)} async-done(((bf16[4,256,128]{1,2,0:T(8,128)(2,1)}), bf16[4,256,128]{1,2,0:T(8,128)(2,1)S(1)}, u32[]{:S(2)}, u32[]{:S(2)}) %all-to-all-start) | async-done | bytes 262176 | tf_op jit(solution)/shard_map/all_to_all | solution.py:25
  92.9 0.8 copy.5
  (1 shorter events, 0.0 us)
Async XLA Ops:
  7.2 2.2 %copy-start = (bf16[256,4096]{1,0:T(8,128)(2,1)S(1)}, bf16[256,4096]{1,0:T(8,128)(2,1)}, u32[]{:S(2)}) copy-start(bf16[256,4096]{1,0:T(8,128)(2,1)} %param.3) | copy-start | bytes 6291460
  7.2 68.9 %all-gather.2.cloned.1.call-start = ((), (), s32[]{:S(2)}) async-start(), calls=%async_computation.1 | async-start | bytes 4325376 | tf_op jit(solution)/shard_map/all_gather | solution.py:22
  83.5 9.4 %all-to-all-start = ((bf16[4,256,128]{1,2,0:T(8,128)(2,1)}), bf16[4,256,128]{1,2,0:T(8,128)(2,1)S(1)}, u32[]{:S(2)}, u32[]{:S(2)}) async-start(bf16[4,256,128]{1,2,0:T(8,128)(2,1)} %bitcast.20), calls=%async_computation | async-start | bytes 524288 | tf_op jit(solution)/shard_map/all_to_all | solution.py:25
Sparse Core Ops, SparseCore 0:
  11.6 64.4 all-gather.1

commit v2 on v1

--- a/solution.py
+++ b/solution.py
@@ -1,13 +1,26 @@
+import functools
+
 import jax
 import jax.numpy as jnp
 from jax import lax
+from jax.experimental import pallas as pl
+from jax.experimental.pallas import tpu as pltpu
 from jax.sharding import PartitionSpec as P
 
-
-def pair_square(left, right):
-    product = lax.dot_general(
+MESH = pl.DeviceIdType.MESH
+ORDERS = ("xzy", "yzx", "zxy", "zyx")
+CHUNKS = len(ORDERS)
+LONGEST_LINE = 4
+
+
+def dot_nt(left, right):
+    return lax.dot_general(
         left, right, (((1,), (1,)), ((), ())), preferred_element_type=jnp.float32
     )
+
+
+def pair_square(left, right):
+    product = dot_nt(left, right)
     return product * product
 
 
@@ -32,9 +45,245 @@
     return (numerators, gram)
 
 
+def kernel(groups, blocks, capacity, cells_ref, count_ref, orb_hbm, num_ref, gram_ref,
+           orb, pts, res, orb_sem, own_sem, recv, precv, zsend, xsend, ysend, psend, rsend, rrecv):
+    g = lax.axis_index("grp")
+    b = lax.axis_index("blk")
+    line = blocks // 2
+    x, c = g // 2, g % 2
+    z, y = b // 2, b % 2
+    rows, width = orb.shape
+    part = width // CHUNKS
+    other_core = x * 2 + 1 - c
+    other_x = (1 - x) * 2 + c
+    far_core = (1 - x) * 2 + 1 - c
+    other_y = z * 2 + 1 - y
+    quarter_len = capacity * blocks
+
+    load = pltpu.make_async_copy(orb_hbm, orb, orb_sem)
+    load.start()
+
+    barrier = pltpu.get_barrier_semaphore()
+
+    def greet(gg, bb):
+        pl.semaphore_signal(barrier, inc=1, device_id={"grp": gg, "blk": bb}, device_id_type=MESH)
+
+    greet(other_core, b)
+    greet(other_x, b)
+    greet(far_core, b)
+    greet(g, other_y)
+
+    @pl.when(z > 0)
+    def _():
+        greet(g, b - 2)
+
+    @pl.when(z < line - 1)
+    def _():
+        greet(g, b + 2)
+
+    load.wait()
+    slot = lax.broadcasted_iota(jnp.int32, (capacity, rows), 0)
+    cell = lax.broadcasted_iota(jnp.int32, (capacity, rows), 1)
+    wanted = jnp.full((capacity, rows), -1, jnp.int32)
+    for j in range(capacity):
+        wanted = jnp.where(slot == j, cells_ref[j], wanted)
+    wanted = jnp.where(slot < count_ref[0], wanted, -1)
+    pick = jnp.where(cell == wanted, 1.0, 0.0).astype(jnp.bfloat16)
+    own_rows = pl.ds(pl.multiple_of((g * blocks + b) * capacity, capacity), capacity)
+    pts[own_rows, :] = jnp.dot(pick, orb[...], preferred_element_type=jnp.float32).astype(jnp.bfloat16)
+
+    inner = (z > 0) & (z < line - 1)
+
+    @pl.when(inner)
+    def _():
+        pl.semaphore_wait(barrier, 6)
+
+    @pl.when(jnp.logical_not(inner))
+    def _():
+        pl.semaphore_wait(barrier, 5)
+
+    def piece(q, core, sz, k):
+        xx = 1 - x if q in (1, 3) else x
+        yy = 1 - y if q in (2, 3) else y
+        owner = (xx * 2 + core) * blocks + sz * 2 + yy
+        return pts.at[pl.ds(pl.multiple_of(owner * capacity, capacity), capacity),
+                      pl.ds(k * part, part)]
+
+    def move(q, sz, k, send_sem, recv_sem, gg, bb):
+        ref = piece(q, c, sz, k)
+        return pltpu.make_async_remote_copy(
+            src_ref=ref, dst_ref=ref, send_sem=send_sem, recv_sem=recv_sem,
+            device_id={"grp": gg, "blk": bb}, device_id_type=MESH)
+
+    def along_z(q, sz, k, way):
+        return move(q, sz, k, zsend.at[(way + 1) // 2, (q + 1) // 2, sz, k], recv.at[q, sz, k],
+                    g, b + 2 * way)
+
+    def over_x(q, sz, k):
+        return move(q, sz, k, xsend.at[q // 2, sz, k], recv.at[q + 1, sz, k], other_x, b)
+
+    def over_y(q, sz, k):
+        return move(q, sz, k, ysend.at[q, sz, k], recv.at[q + 2, sz, k], g, other_y)
+
+    def to_core(q, sz, k):
+        return move(q, sz, k, psend.at[q, sz, k], precv.at[q, sz, k], other_core, b)
+
+    def arrived(q, sz, k):
+        ref = piece(q, c, sz, k)
+        pltpu.make_async_copy(ref, ref, recv.at[q, sz, k]).wait()
+
+    def core_arrived(q, sz, k):
+        ref = piece(q, 1 - c, sz, k)
+        pltpu.make_async_copy(ref, ref, precv.at[q, sz, k]).wait()
+
+    def sends(q, sz, k, sign, act):
+        done = {0: "", 1: "x", 2: "y", 3: "xy"}[q] + ("z" if sign != 0 else "")
+        reached = max([ORDERS[k].index(d) for d in done], default=-1)
+        later = ORDERS[k][reached + 1:]
+        down_too = ("z" in later) or (done != "" and ORDERS[k][reached] == "z" and sign > 0)
+        up_too = ("z" in later) or (done != "" and ORDERS[k][reached] == "z" and sign < 0)
+        if down_too:
+            @pl.when(z > 0)
+            def _():
+                act(along_z(q, sz, k, -1))
+        if up_too:
+            @pl.when(z < line - 1)
+            def _():
+                act(along_z(q, sz, k, 1))
+        if "x" in later:
+            act(over_x(q, sz, k))
+        if "y" in later:
+            act(over_y(q, sz, k))
+        act(to_core(q, sz, k))
+
+    def take(q, sz, k, sign):
+        if q != 0 or sign != 0:
+            arrived(q, sz, k)
+        sends(q, sz, k, sign, lambda copy: copy.start())
+
+    def sent(q, sz, k, sign):
+        sends(q, sz, k, sign, lambda copy: copy.wait_send())
+
+    def walk(act, wave):
+        for stage, quadrants in enumerate(((0,), (1, 2), (3,))):
+            s = wave - stage
+            if s < 0 or s > line - 1:
+                continue
+            for k in range(CHUNKS):
+                for sign in ((0,) if s == 0 else (1, -1)):
+                    sz = z + sign * s
+
+                    def both(sz=sz, k=k, sign=sign):
+                        for q in quadrants:
+                            act(q, sz, k, sign)
+
+                    if sign == 0:
+                        both()
+                    elif sign > 0:
+                        pl.when(z + s < line)(both)
+                    else:
+                        pl.when(z - s >= 0)(both)
+
+    def squares(xx):
+        points = pts[pl.ds(pl.multiple_of(xx * 2 * quarter_len, capacity), 2 * quarter_len), :]
+        return pair_square(orb[...], points).astype(jnp.bfloat16)
+
+    def result_copy(i, gg):
+        return pltpu.make_async_remote_copy(
+            src_ref=res.at[i],
+            dst_ref=num_ref.at[pl.ds(pl.multiple_of(g * rows, rows), rows), :],
+            send_sem=rsend.at[i], recv_sem=rrecv.at[i],
+            device_id={"grp": gg, "blk": b}, device_id_type=MESH)
+
+    def own_result():
+        return pltpu.make_async_copy(
+            res.at[0], num_ref.at[pl.ds(pl.multiple_of(g * rows, rows), rows), :], own_sem)
+
+    for wave in range(line + 2):
+        walk(take, wave)
+        if wave == line:
+            for q in (0, 2, 1):
+                for sz in range(line):
+                    for k in range(CHUNKS):
+                        core_arrived(q, sz, k)
+            near = squares(x)
+            first = near[:, :quarter_len]
+            second = near[:, quarter_len:]
+            res[0] = jnp.where(c == 0, first, second)
+            res[1] = jnp.where(c == 0, second, first)
+            quarter = pts[pl.ds(pl.multiple_of(g * quarter_len, quarter_len), quarter_len), :]
+            across = jnp.concatenate(
+                [pts[pl.ds(pl.multiple_of((a * blocks + b) * capacity, capacity), capacity), :]
+                 for a in range(groups)], axis=0)
+            gram_ref[...] = pair_square(across, quarter).reshape(groups, capacity, quarter_len)
+            own_result().start()
+            result_copy(1, other_core).start()
+
+    for sz in range(line):
+        for k in range(CHUNKS):
+            core_arrived(3, sz, k)
+    far = squares(1 - x)
+    first = far[:, :quarter_len]
+    second = far[:, quarter_len:]
+    res[2] = jnp.where(c == 0, first, second)
+    res[3] = jnp.where(c == 0, second, first)
+    result_copy(2, other_x).start()
+    result_copy(3, far_core).start()
+
+    for wave in range(line + 2):
+        walk(sent, wave)
+    own_result().wait()
+    for i, gg in ((1, other_core), (2, other_x), (3, far_core)):
+        result_copy(i, gg).wait_send()
+        spot = num_ref.at[pl.ds(pl.multiple_of(gg * rows, rows), rows), :]
+        pltpu.make_async_copy(spot, spot, rrecv.at[i]).wait()
+
+
+def per_device_kernel(orbitals, point_cells, point_count):
+    cells, width = orbitals.shape
+    capacity = point_cells.shape[0]
+    groups = lax.axis_size("grp")
+    blocks = lax.axis_size("blk")
+    line = blocks // 2
+    quarter_len = capacity * blocks
+    dma = pltpu.SemaphoreType.DMA
+    return pl.pallas_call(
+        functools.partial(kernel, groups, blocks, capacity),
+        out_shape=(
+            jax.ShapeDtypeStruct((groups * cells, quarter_len), jnp.bfloat16),
+            jax.ShapeDtypeStruct((groups, capacity, quarter_len), jnp.float32),
+        ),
+        in_specs=[
+            pl.BlockSpec(memory_space=pltpu.SMEM),
+            pl.BlockSpec(memory_space=pltpu.SMEM),
+            pl.BlockSpec(memory_space=pltpu.HBM),
+        ],
+        out_specs=(
+            pl.BlockSpec(memory_space=pl.ANY),
+            pl.BlockSpec(memory_space=pltpu.VMEM),
+        ),
+        scratch_shapes=[
+            pltpu.VMEM((cells, width), jnp.bfloat16),
+            pltpu.VMEM((groups * quarter_len, width), jnp.bfloat16),
+            pltpu.VMEM((groups, cells, quarter_len), jnp.bfloat16),
+            dma, dma,
+            dma((4, line, CHUNKS)), dma((4, line, CHUNKS)),
+            dma((2, 2, line, CHUNKS)), dma((2, line, CHUNKS)), dma((2, line, CHUNKS)),
+            dma((4, line, CHUNKS)),
+            dma((groups,)), dma((groups,)),
+        ],
+        compiler_params=pltpu.CompilerParams(
+            collective_id=0, has_side_effects=True, vmem_limit_bytes=62 * 1024 * 1024 + 512 * 1024
+        ),
+    )(point_cells, point_count, orbitals)
+
+
 def solution(mesh):
     in_specs = (P(("blk", "grp"), None), P(("grp", "blk")), P(("grp", "blk")))
     out_specs = (P("blk", "grp"), P(None, "blk", "grp"))
+    groups, blocks = mesh.shape["grp"], mesh.shape["blk"]
+    fits = groups == 4 and blocks % 2 == 0 and 2 <= blocks // 2 <= LONGEST_LINE
     return jax.shard_map(
-        per_device, mesh=mesh, in_specs=in_specs, out_specs=out_specs, check_vma=False
+        per_device_kernel if fits else per_device,
+        mesh=mesh, in_specs=in_specs, out_specs=out_specs, check_vma=False
     )

time: 101 us -> 39.5 us (0.39)
  waiting for transfers between devices: 69.2 us -> 0 us
  Pallas kernels: 0 us -> 34.9 us
  between operations: 14.9 us -> 1.28 us
  matrix products: 6.31 us -> 0 us
  starting transfers between devices: 3.44 us -> 0 us
  other arithmetic: 2.07 us -> 0 us
  local copies, waits for them, and re-layouts: 4.66 us -> 3.04 us
    all_gather x1 -> x0, waiting for transfers between devices: 65.4 us -> none  [per_device(): points = lax.all_gather(own_points, ('grp', 'blk'), axis=0, tiled=True)]
    pallas_call x0 -> x1, Pallas kernels: none -> 34.9 us  [per_device_kernel(): pl.pallas_call(functools.partial(kernel, groups, blocks, capacity), out_s...]
    dot_general x2 -> x0, matrix products: 6.31 us -> none  [pair_square(): lax.dot_general(left, right, (((1,), (1,)), ((), ())), preferred_element_...]
    all_to_all x1 -> x0, waiting for transfers between devices: 3.83 us -> none  [per_device(): lax.all_to_all(mine, 'grp', 0, 0, tiled=True)]
    all_to_all x1 -> x0, starting transfers between devices: 3.41 us -> none  [per_device(): lax.all_to_all(mine, 'grp', 0, 0, tiled=True)]
    dynamic_slice x2 -> x0, local copies, waits for them, and re-layouts: 3.18 us -> none  [the longest x1 1.89 us: per_device(): lax.dynamic_index_in_dim(by_owner, lax.axis_index('blk'), 1, keepdims=False)]
    unnamed x2, local copies, waits for them, and re-layouts: 0.01 us -> 3.04 us
  transfers between devices with their start and end apart: 2 -> 0, of which waited for: 2 -> 0; matrix products, arithmetic and copies ran while one was open for 2% -> 0% of each run, Pallas kernels for 0% -> 0%
where the time goes in v2:
time: 39.5 us; the launch traced here: 39.3 us
  Pallas kernels  34.9 us (88%)
  local copies, waits for them, and re-layouts  3.04 us (8%)
  between operations  1.28 us (3%)
    pallas_call x1, Pallas kernels, per_device_kernel(): pl.pallas_call(functools.partial(kernel, groups, blocks, capacity), out_s...  34.9 us
    unnamed x2, local copies, waits for them, and re-layouts  3.04 us

profile of v2, /device:TPU:0, one launch (start us, length us, event | category | flops | bytes accessed | tf_op | source)
XLA Modules:
  0.0 39.3 jit_solution(14395073375063219879)
XLA Ops:
  1.3 34.9 %shard_map.50 = (bf16[1024,128]{1,0:T(8,128)(2,1)}, f32[4,16,128]{2,1,0:T(8,128)}) custom-call(s32[16]{0:T(128)} %cells_ref.1, s32[1]{0:T(128)S(6)} %copy.7.count_ref, bf16[256,4096]{1,0:T(8,128)(2,1)} %orb_hbm.1), custom_call_target="tpu_custom_call" | custom-call | tf_op jit(solution)/shard_map/pallas_call | solution.py:250
  36.2 1.7 %copy.8 = bf16[1024,128]{1,0:T(8,128)(2,1)} copy(bf16[1024,128]{1,0:T(8,128)(2,1)} %get-tuple-element.4) | data formatting | bytes 524288
  37.9 1.4 %copy.9 = f32[4,16,128]{2,1,0:T(8,128)} copy(f32[4,16,128]{2,1,0:T(8,128)} %get-tuple-element.5) | data formatting | bytes 65536

commit v3 on v2

--- a/solution.py
+++ b/solution.py
@@ -8,7 +8,7 @@
 from jax.sharding import PartitionSpec as P
 
 MESH = pl.DeviceIdType.MESH
-ORDERS = ("xzy", "yzx", "zxy", "zyx")
+ORDERS = ("zxy", "zyx")
 CHUNKS = len(ORDERS)
 LONGEST_LINE = 4
 
@@ -45,8 +45,8 @@
     return (numerators, gram)
 
 
-def kernel(groups, blocks, capacity, cells_ref, count_ref, orb_hbm, num_ref, gram_ref,
-           orb, pts, res, orb_sem, own_sem, recv, precv, zsend, xsend, ysend, psend, rsend, rrecv):
+def kernel(groups, blocks, capacity, cells_ref, count_ref, orb, num_ref, gram_ref,
+           pts, res, own_sem, recv, precv, zsend, xsend, ysend, psend, rsend, rrecv):
     g = lax.axis_index("grp")
     b = lax.axis_index("blk")
     line = blocks // 2
@@ -60,9 +60,6 @@
     other_y = z * 2 + 1 - y
     quarter_len = capacity * blocks
 
-    load = pltpu.make_async_copy(orb_hbm, orb, orb_sem)
-    load.start()
-
     barrier = pltpu.get_barrier_semaphore()
 
     def greet(gg, bb):
@@ -81,7 +78,6 @@
     def _():
         greet(g, b + 2)
 
-    load.wait()
     slot = lax.broadcasted_iota(jnp.int32, (capacity, rows), 0)
     cell = lax.broadcasted_iota(jnp.int32, (capacity, rows), 1)
     wanted = jnp.full((capacity, rows), -1, jnp.int32)
@@ -256,24 +252,23 @@
         in_specs=[
             pl.BlockSpec(memory_space=pltpu.SMEM),
             pl.BlockSpec(memory_space=pltpu.SMEM),
-            pl.BlockSpec(memory_space=pltpu.HBM),
+            pl.BlockSpec(memory_space=pltpu.VMEM),
         ],
         out_specs=(
             pl.BlockSpec(memory_space=pl.ANY),
             pl.BlockSpec(memory_space=pltpu.VMEM),
         ),
         scratch_shapes=[
-            pltpu.VMEM((cells, width), jnp.bfloat16),
             pltpu.VMEM((groups * quarter_len, width), jnp.bfloat16),
             pltpu.VMEM((groups, cells, quarter_len), jnp.bfloat16),
-            dma, dma,
+            dma,
             dma((4, line, CHUNKS)), dma((4, line, CHUNKS)),
             dma((2, 2, line, CHUNKS)), dma((2, line, CHUNKS)), dma((2, line, CHUNKS)),
             dma((4, line, CHUNKS)),
             dma((groups,)), dma((groups,)),
         ],
         compiler_params=pltpu.CompilerParams(
-            collective_id=0, has_side_effects=True, vmem_limit_bytes=62 * 1024 * 1024 + 512 * 1024
+            collective_id=0, has_side_effects=True, vmem_limit_bytes=48 * 1024 * 1024
         ),
     )(point_cells, point_count, orbitals)
 

time: 39.5 us -> 38.7 us (0.980)
  Pallas kernels: 34.9 us -> 33.7 us
  local copies, waits for them, and re-layouts: 3.04 us -> 3.56 us
    pallas_call x1, Pallas kernels: 34.9 us -> 33.7 us  [per_device_kernel(): pl.pallas_call(functools.partial(kernel, groups, blocks, capacity), out_s...]
    unnamed x2 -> x6, local copies, waits for them, and re-layouts: 3.04 us -> 3.56 us
where the time goes in v3:
time: 38.7 us; the launch traced here: 38.5 us
  Pallas kernels  33.7 us (87%)
  local copies, waits for them, and re-layouts  3.56 us (9%)
  between operations  1.29 us (3%)
    pallas_call x1, Pallas kernels, per_device_kernel(): pl.pallas_call(functools.partial(kernel, groups, blocks, capacity), out_s...  33.7 us
    unnamed x6, local copies, waits for them, and re-layouts  3.56 us

profile of v3, /device:TPU:0, one launch (start us, length us, event | category | flops | bytes accessed | tf_op | source)
XLA Modules:
  0.0 38.5 jit_solution(1480747524828331944)
XLA Ops:
  1.3 0.0 copy-start
  1.3 1.6 %copy-done = bf16[256,4096]{1,0:T(8,128)(2,1)S(1)} copy-done((bf16[256,4096]{1,0:T(8,128)(2,1)S(1)}, bf16[256,4096]{1,0:T(8,128)(2,1)}, u32[]{:S(2)}) %copy-start) | copy-done | bytes 2097176
  2.9 0.0 copy-start.1
  2.9 0.7 %copy-done.1 = s32[16]{0:T(128)S(1)} copy-done((s32[16]{0:T(128)S(1)}, s32[16]{0:T(128)}, u32[]{:S(2)}) %copy-start.1) | copy-done | bytes 88
  3.5 33.7 %shard_map.50 = (bf16[1024,128]{1,0:T(8,128)(2,1)S(1)}, f32[4,16,128]{2,1,0:T(8,128)S(1)}) custom-call(s32[16]{0:T(128)S(1)} %copy-done.1, s32[1]{0:T(128)S(6)} %copy.7.count_ref, bf16[256,4096]{1,0:T(8,128)(2,1)S(1)} %copy-done), custom_call_target="tpu_custom_call" | custom-call | tf_op jit(solution)/shard_map/pallas_call | solution.py:246
  37.2 0.7 %copy.8 = bf16[1024,128]{1,0:T(8,128)(2,1)} copy(bf16[1024,128]{1,0:T(8,128)(2,1)S(1)} %get-tuple-element.4) | data formatting | bytes 524288
  37.9 0.6 %copy.9 = f32[4,16,128]{2,1,0:T(8,128)} copy(f32[4,16,128]{2,1,0:T(8,128)S(1)} %get-tuple-element.5) | data formatting | bytes 65536
Async XLA Ops:
  1.3 1.6 %copy-start = (bf16[256,4096]{1,0:T(8,128)(2,1)S(1)}, bf16[256,4096]{1,0:T(8,128)(2,1)}, u32[]{:S(2)}) copy-start(bf16[256,4096]{1,0:T(8,128)(2,1)} %orb.1) | copy-start | bytes 6291460
  2.9 0.7 %copy-start.1 = (s32[16]{0:T(128)S(1)}, s32[16]{0:T(128)}, u32[]{:S(2)}) copy-start(s32[16]{0:T(128)} %cells_ref.1) | copy-start | bytes 196
